TPU v7x, 32 devices: a whole 2x2x4 slice. The times are simulated.
32 devices in a mesh: band: 8 (over y, x, core), lev: 4 (over z).
Axes of the slice: x: 2, y: 2, z: 4, core: 2. Of those that a mesh axis runs over, the one named last changes fastest.
Arguments:
- pattern: float32 [1024, 128], P('band'), may hold values from -3 to 3
- taper: float32 [136], P('lev'), may hold values from 0.1 to 1
- thickness: float32 [136], P('lev'), may hold values from 0.2 to 2
- block_source: int32 [1024], P('band'), may hold values from 0 to 1023, as said below
- tendencies: bfloat16 [4, 136, 131072], P(None, 'lev', 'band'), may hold values from -6 to 6
Outputs:
- perturbed: bfloat16 [4, 136, 131072], P(None, 'lev', 'band')
- integrals: float32 [2, 131072], P(None, 'band')
Inputs may be any that keep to these rules, and one draw needn't show every extreme that they name: block_source is a permutation of 0 to 1023; the 128 physics blocks of each band index take exactly 128 // 8 grid blocks from the 128 grid blocks of each band index.
All inputs are finite; a program needn't handle non-finite values.
Results may differ from a plain program's by a relative error of at most 0.001.
Values sent between devices are 32-bit elements; how exact they have to be, the bound alone decides.
A program may use at most 64 MiB of HBM per device.

v0:
```python
import jax
import jax.numpy as jnp
from jax import lax
from jax.sharding import PartitionSpec as P


def body(pattern, taper, thickness, block_source, tendencies):
    clipped = jnp.tanh(pattern)
    whole = lax.all_gather(clipped, "band", axis=0, tiled=True)
    local = jnp.take(whole, block_source, axis=0).reshape(-1)
    pert = taper[:, None] * local[None, :]
    perturbed = (tendencies.astype(jnp.float32) * (1.0 + pert)[None, :, :]).astype(jnp.bfloat16)
    moist = tendencies[2:4].astype(jnp.float32)
    partial_sums = jnp.sum(thickness[None, :, None] * moist * pert[None, :, :], axis=1)
    column_total, squares = lax.psum((partial_sums, jnp.sum(thickness * thickness)), "lev")
    integrals = column_total / jnp.sqrt(squares)
    return (perturbed, integrals)


def solution(mesh):
    in_specs = (P("band", None), P("lev"), P("lev"), P("band"), P(None, "lev", "band"))
    out_specs = (P(None, "lev", "band"), P(None, "band"))
    return jax.shard_map(body, mesh=mesh, in_specs=in_specs, out_specs=out_specs, check_vma=False)
```

profile of v0, /device:TPU:0, one launch (start us, length us, event | category | flops | bytes accessed | tf_op | source)
XLA Modules:
  0.0 72.4 jit_solution(15371106237540076167)
XLA Ops:
  7.2 0.0 copy-start.1
  7.2 0.0 all-reduce.2.cloned.1.call-start
  7.2 0.7 compare_and_fusion
  7.9 0.7 compare_select_fusion
  8.6 0.9 %tanh.3 = f32[128,128]{1,0:T(8,128)S(1)} tanh(f32[128,128]{1,0:T(8,128)} %param.5) | non-fusion elementwise | bytes 131072 | tf_op jit(solution)/shard_map/tanh | solution.py:8
  9.4 11.3 %all_gather.3 = f32[1024,128]{1,0:T(8,128)S(1)} all-gather(f32[128,128]{1,0:T(8,128)S(1)} %tanh.3), channel_id=1, replica_groups=mesh['band'=8,'lev'=4] {'band'}, dimensions={0}, use_global_device_ids=true | all-gather | bytes 589824 | tf_op jit(solution)/shard_map/all_gather | solution.py:9
  20.7 0.6 gather_fusion
  21.4 0.0 copy-start
  21.4 0.1 select_bitcast_fusion
  21.5 1.2 %broadcast_multiply_fusion = (f32[34,16384]{1,0:T(8,128)S(1)}, f32[34,16384]{1,0:T(8,128)S(1)}) fusion(f32[16384]{0:T(1024)S(1)} %select_bitcast_fusion, f32[34]{0:T(128)} %param.6), kind=kLoop, calls=%fused_computation.4 | loop fusion | flops 1114112 | bytes 4522120 | tf_op jit(solution)/shard_map/mul | solution.py:11
  22.7 0.0 copy-done.1
  22.7 1.0 %copy-done = bf16[4,34,16384]{2,0,1:T(4,128)(2,1)S(1)} copy-done((bf16[4,34,16384]{2,0,1:T(4,128)(2,1)S(1)}, bf16[4,34,16384]{2,0,1:T(4,128)(2,1)}, u32[]{:S(2)}) %copy-start) | copy-done | bytes 4456472
  23.7 5.1 %multiply_reduce_fusion = f32[2,16384]{1,0:T(2,128)} fusion(f32[34]{0:T(128)S(1)} %copy-done.1, f32[34,16384]{1,0:T(8,128)S(1)} %get-tuple-element.2, bf16[4,34,16384]{2,0,1:T(4,128)(2,1)S(1)} %copy-done), kind=kLoop, calls=%fused_computation.2 | loop fusion | flops 4423680 | bytes 4587656 | tf_op jit(solution)/shard_map/reduce_sum | solution.py:14
  28.8 0.0 all-reduce.2.cloned.1.call-update
  28.8 0.6 multiply_reduce_fusion.1
  29.4 7.8 %multiply_convert_fusion = bf16[4,34,16384]{2,0,1:T(4,128)(2,1)} fusion(bf16[4,34,16384]{2,0,1:T(4,128)(2,1)} %param.9, f32[34,16384]{1,0:T(8,128)S(1)} %get-tuple-element.3), kind=kLoop, calls=%fused_computation.1 | loop fusion | flops 6684672 | bytes 11141120 | tf_op jit(solution)/shard_map/convert_element_type | solution.py:12
  37.2 12.6 %psum.15 = f32[]{:T(128)} all-reduce(f32[]{:T(128)} %multiply_reduce_fusion.1), channel_id=1, replica_groups=mesh['band'=8,'lev'=4] {'lev'}, use_global_device_ids=true, to_apply=%region_3.4 | all-reduce | flops 1 | bytes 8 | tf_op jit(solution)/shard_map/psum | solution.py:15
  50.4 13.5 %all-reduce.2.cloned.1.call-done = f32[2,16384]{1,0:T(2,128)} async-done(((f32[2,16384]{1,0:T(2,128)}), f32[2,16384]{1,0:T(2,128)}) %all-reduce.2.cloned.1.call-update) | async-done | bytes 131088 | tf_op jit(solution)/shard_map/psum | solution.py:15
  63.9 1.6 %broadcast_divide_fusion = f32[2,16384]{1,0:T(2,128)} fusion(f32[2,16384]{1,0:T(2,128)} %all-reduce.2.cloned.1.call-done, f32[]{:T(128)S(6)} %sqrt.3), kind=kLoop, calls=%fused_computation.5 | loop fusion | flops 32768 | bytes 262148 | tf_op jit(solution)/shard_map/div | solution.py:16
  (1 shorter events, 0.0 us)
Async XLA Ops:
  7.2 15.5 %copy-start.1 = (f32[34]{0:T(128)S(1)}, f32[34]{0:T(128)}, u32[]{:S(2)}) copy-start(f32[34]{0:T(128)} %param.7) | copy-start | bytes 412
  7.2 56.8 %all-reduce.2.cloned.1.call-start = ((), (), s32[]{:S(2)}) async-start(), calls=%async_computation | async-start | bytes 262144 | tf_op jit(solution)/shard_map/psum | solution.py:15
  21.4 2.3 %copy-start = (bf16[4,34,16384]{2,0,1:T(4,128)(2,1)S(1)}, bf16[4,34,16384]{2,0,1:T(4,128)(2,1)}, u32[]{:S(2)}) copy-start(bf16[4,34,16384]{2,0,1:T(4,128)(2,1)} %param.9) | copy-start | bytes 13369348
Sparse Core Ops, SparseCore 0:
  28.9 34.9 all-reduce.1
where the time goes:
time: 72.7 us; the launch traced here: 72.4 us
  blocking collectives  24 us (33%)
  other arithmetic  17.7 us (24%)
  between operations  14.7 us (20%)
  waiting for transfers between devices  13.5 us (19%)
  local copies, waits for them, and re-layouts  2.46 us (3%)
    psum x1, waiting for transfers between devices, body(): lax.psum((partial_sums, jnp.sum(thickness * thickness)), 'lev')  13.5 us
    psum x1, blocking collectives, body(): lax.psum((partial_sums, jnp.sum(thickness * thickness)), 'lev')  12.6 us
    all_gather x1, blocking collectives, body(): whole = lax.all_gather(clipped, 'band', axis=0, tiled=True)  11.3 us
    convert_element_type x1, other arithmetic, body(): (tendencies.astype(jnp.float32) * (1.0 + pert)[None, :, :]).astype(jnp.bf...  7.81 us
    reduce_sum x1, other arithmetic, body(): jnp.sum(thickness[None, :, None] * moist * pert[None, :, :], axis=1)  5.11 us
    div x1, other arithmetic, body(): integrals = column_total / jnp.sqrt(squares)  1.6 us
  transfers between devices with their start and end apart: 1, of which 1 were waited for; matrix products, arithmetic and copies ran while one was open for 12% of the time, Pallas kernels for 0%

commit v1 on v0

v1 whole, which is shorter than its diff:
```python
import functools
import jax
import jax.numpy as jnp
from jax import lax
from jax.experimental import pallas as pl
from jax.experimental.pallas import tpu as pltpu
from jax.sharding import PartitionSpec as P

MESH = pl.DeviceIdType.MESH


def exchange(n_band, n_lev, pattern, source_hbm, taper_hbm, thickness_hbm, tend, held, spread, totals,
             whole, acc, part, inbox, source, taper, thickness, small_sem, own_sem, load_sem, out_sem, in_sem, pass_sem, got_sem,
             part_send, part_recv, total_send, total_recv):
    band, lev = lax.axis_index("band"), lax.axis_index("lev")
    levels, rows, lanes = tend.shape
    blocks = pattern.shape[0]
    fields = rows // blocks
    share, piece = blocks // n_lev, rows // n_lev
    pairs = n_band // 2
    pair, core = band // 2, band % 2
    mate = pair * 2 + 1 - core

    def chunk_of(step):
        return lax.rem(lev + 1 + step, n_lev)

    def load(step):
        span = pl.ds(pl.multiple_of(chunk_of(step) * piece, piece), piece)
        return pltpu.make_async_copy(tend.at[:, span, :], held.at[:, span, :], load_sem.at[step])

    def block_rows(who):
        return pl.ds(pl.multiple_of(who * blocks, blocks), blocks)

    own = pltpu.make_async_copy(pattern, whole.at[block_rows(band)], own_sem)
    own.start()
    small = [pltpu.make_async_copy(a, b, small_sem.at[i]) for i, (a, b) in enumerate(
        ((thickness_hbm, thickness), (taper_hbm, taper), (source_hbm, source)))]
    for copy in small:
        copy.start()
    for step in range(n_lev):
        load(step).start()

    barrier = pltpu.get_barrier_semaphore()
    pl.semaphore_signal(barrier, inc=1, device_id={"band": mate}, device_id_type=MESH)
    for d in range(1, pairs):
        peer = lax.rem(pair + d, pairs) * 2 + core
        pl.semaphore_signal(barrier, inc=1, device_id={"band": peer}, device_id_type=MESH)
    for d in range(1, n_lev):
        pl.semaphore_signal(barrier, inc=1, device_id={"lev": lax.rem(lev + d, n_lev)}, device_id_type=MESH)
    own.wait()
    pl.semaphore_wait(barrier, pairs + n_lev - 1)

    def direct(d):
        peer = lax.rem(pair + d, pairs) * 2 + core
        mine = whole.at[block_rows(band)]
        return pltpu.make_async_remote_copy(mine, mine, out_sem.at[d], in_sem.at[d],
                                            device_id={"band": peer}, device_id_type=MESH)

    def relay(d):
        origin = lax.rem(pair - d + pairs, pairs) * 2 + core
        block = whole.at[block_rows(origin)]
        return pltpu.make_async_remote_copy(block, block, pass_sem.at[d], got_sem.at[d],
                                            device_id={"band": mate}, device_id_type=MESH)

    for d in range(1, pairs):
        direct(d).start()
    relay(0).start()

    for copy in small:
        copy.wait()
    squares = thickness[0] * thickness[0]
    for l in range(1, levels):
        squares += thickness[l] * thickness[l]

    def give(step):
        owner = chunk_of(step)
        return pltpu.make_async_remote_copy(part.at[step], inbox.at[n_lev - 2 - step], part_send.at[step],
                                            part_recv.at[n_lev - 2 - step],
                                            device_id={"lev": owner}, device_id_type=MESH)

    for step in range(n_lev):
        load(step).wait()
        first = pl.multiple_of(chunk_of(step) * piece, piece)
        for r in range(0, piece, 64):
            def add(l, total):
                weight = thickness[l] * taper[l]
                return total + weight * held[l, pl.ds(first + r, 64), :].astype(jnp.float32)
            acc[pl.ds(r, 64), :] = lax.fori_loop(0, levels, add, jnp.zeros((64, lanes), jnp.float32), unroll=2)
        for k in range(2):
            part[step, k * share:(k + 1) * share, :] = acc[pl.ds(fields - 2 + k, share, stride=fields), :]
        part[step, 2 * share:, :] = jnp.full((8, lanes), squares, jnp.float32)
        if step < n_lev - 1:
            give(step).start()

    def arrived(d):
        direct(d).wait_recv()
        relay(d).start()

    for d in range(1, pairs):
        arrived(d)

    for step in range(n_lev - 1):
        give(step).wait()
    total = part[n_lev - 1]
    for slot in range(n_lev - 1):
        total = total + inbox[slot]
    totals[lev] = total[:2 * share] / jnp.sqrt(total[2 * share:2 * share + 1])

    def publish(d):
        return pltpu.make_async_remote_copy(totals.at[lev], totals.at[lev], total_send.at[d], total_recv.at[d],
                                            device_id={"lev": lax.rem(lev + d, n_lev)}, device_id_type=MESH)

    for d in range(1, n_lev):
        publish(d).start()

    for d in range(pairs):
        relay(d).wait()
    for d in range(1, pairs):
        direct(d).wait_send()

    def pick(j, _):
        row = whole[pl.ds(source[j], 1), :]
        acc[pl.ds(j, 1), :] = row
        return 0

    lax.fori_loop(0, blocks, pick, 0, unroll=8)
    local = jnp.tanh(acc[0:blocks, :])
    for f in range(fields):
        spread[pl.ds(f, blocks, stride=fields), :] = local

    for d in range(1, n_lev):
        publish(d).wait()


def scale(n_lev, taper, held, spread, totals, out, column, made, sums, out_sem, sum_sem):
    levels, rows, lanes = held.shape
    blocks = column.shape[0]
    share, fields = blocks // n_lev, rows // blocks

    def level(l, _):
        for r in range(0, rows, 64):
            factor = 1.0 + taper[l] * spread[pl.ds(r, 64), :]
            made[l, pl.ds(r, 64), :] = (held[l, pl.ds(r, 64), :].astype(jnp.float32) * factor).astype(made.dtype)
        pltpu.make_async_copy(made.at[l], out.at[l], out_sem.at[l]).start()
        return 0

    lax.fori_loop(0, levels, level, 0)
    for c in range(n_lev):
        local = spread[pl.ds(c * share * fields, share, stride=fields), :]
        for k in range(2):
            sums[c * share:(c + 1) * share, k, :] = totals[c, k * share:(k + 1) * share, :] * local
    done = pltpu.make_async_copy(sums, column, sum_sem)
    done.start()

    def finish(l, _):
        pltpu.make_async_copy(made.at[l], out.at[l], out_sem.at[l]).wait()
        return 0

    lax.fori_loop(0, levels, finish, 0)
    done.wait()


def body(n_band, n_lev, pattern, taper, thickness, block_source, tendencies):
    fields, levels, columns = tendencies.shape
    blocks, lanes = pattern.shape
    rows = blocks * fields
    share, piece, pairs = blocks // n_lev, rows // n_lev, n_band // 2
    tend = tendencies.transpose(1, 0, 2).reshape(levels, fields, blocks, lanes)
    tend = tend.transpose(0, 2, 1, 3).reshape(levels, rows, lanes)
    anywhere = pl.BlockSpec(memory_space=pl.ANY)
    hbm = pl.BlockSpec(memory_space=pltpu.HBM)
    scalars = pl.BlockSpec(memory_space=pltpu.SMEM)
    vector = pl.BlockSpec(memory_space=pltpu.VMEM)
    f32, dma = jnp.float32, pltpu.SemaphoreType.DMA
    held, spread, totals = pl.pallas_call(
        functools.partial(exchange, n_band, n_lev),
        name="exchange",
        out_shape=(pltpu.VMEM(tend.shape, tend.dtype), pltpu.VMEM((rows, lanes), f32),
                   pltpu.VMEM((n_lev, 2 * share, lanes), f32)),
        in_specs=[hbm] * 5,
        out_specs=(vector, vector, vector),
        scratch_shapes=[
            pltpu.VMEM((n_band * blocks, lanes), f32),
            pltpu.VMEM((max(piece, blocks), lanes), f32),
            pltpu.VMEM((n_lev, 2 * share + 8, lanes), f32),
            pltpu.VMEM((n_lev - 1, 2 * share + 8, lanes), f32),
            pltpu.SMEM(block_source.shape, jnp.int32), pltpu.SMEM(taper.shape, f32),
            pltpu.SMEM(thickness.shape, f32), dma((3,)),
            dma, dma((n_lev,)), dma((pairs,)), dma((pairs,)), dma((pairs,)), dma((pairs,)),
            dma((n_lev,)), dma((n_lev,)), dma((n_lev,)), dma((n_lev,)),
        ],
        compiler_params=pltpu.CompilerParams(collective_id=0, has_side_effects=True, vmem_limit_bytes=12 << 20),
    )(*(pltpu.with_memory_space_constraint(x, pltpu.MemorySpace.HBM)
        for x in (pattern, block_source, taper, thickness, tend)))
    in_vmem = lambda x: pltpu.with_memory_space_constraint(x, pltpu.MemorySpace.VMEM)
    out, column = pl.pallas_call(
        functools.partial(scale, n_lev),
        name="scale",
        out_shape=(jax.ShapeDtypeStruct(tend.shape, tend.dtype), jax.ShapeDtypeStruct((blocks, 2, lanes), f32)),
        in_specs=[scalars, vector, vector, vector],
        out_specs=(anywhere, anywhere),
        scratch_shapes=[pltpu.VMEM(tend.shape, tend.dtype), pltpu.VMEM((blocks, 2, lanes), f32), dma((levels,)), dma],
        compiler_params=pltpu.CompilerParams(vmem_limit_bytes=24 << 20),
    )(taper, in_vmem(held), in_vmem(spread), in_vmem(totals))
    out = out.reshape(levels, blocks, fields, lanes).transpose(2, 0, 1, 3).reshape(fields, levels, columns)
    return out, column.transpose(1, 0, 2).reshape(2, columns)


def solution(mesh):
    in_specs = (P("band", None), P("lev"), P("lev"), P("band"), P(None, "lev", "band"))
    out_specs = (P(None, "lev", "band"), P(None, "band"))
    run = functools.partial(body, mesh.shape["band"], mesh.shape["lev"])
    return jax.shard_map(run, mesh=mesh, in_specs=in_specs, out_specs=out_specs, check_vma=False)
```

time: 72.7 us -> 18.7 us (0.26)
  blocking collectives: 24 us -> 0 us
  Pallas kernels: 0 us -> 17.9 us
  other arithmetic: 17.7 us -> 0 us
  between operations: 14.7 us -> 0.65 us
  waiting for transfers between devices: 13.5 us -> 0 us
  local copies, waits for them, and re-layouts: 2.46 us -> 0.01 us
    pallas_call x0 -> x2, Pallas kernels: none -> 17.9 us  [the longest x1 14.8 us: body(): pl.pallas_call(functools.partial(exchange, n_band, n_lev), name='exchange...]
    psum x1 -> x0, waiting for transfers between devices: 13.5 us -> none  [body(): lax.psum((partial_sums, jnp.sum(thickness * thickness)), 'lev')]
    psum x1 -> x0, blocking collectives: 12.6 us -> none  [body(): lax.psum((partial_sums, jnp.sum(thickness * thickness)), 'lev')]
    all_gather x1 -> x0, blocking collectives: 11.3 us -> none  [body(): whole = lax.all_gather(clipped, 'band', axis=0, tiled=True)]
    convert_element_type x1 -> x0, other arithmetic: 7.81 us -> none  [body(): (tendencies.astype(jnp.float32) * (1.0 + pert)[None, :, :]).astype(jnp.bf...]
    reduce_sum x2 -> x0, other arithmetic: 5.7 us -> none  [the longest x1 5.11 us: body(): jnp.sum(thickness[None, :, None] * moist * pert[None, :, :], axis=1)]
    div x1 -> x0, other arithmetic: 1.6 us -> none  [body(): integrals = column_total / jnp.sqrt(squares)]
    mul x1 -> x0, other arithmetic: 1.21 us -> none  [body(): pert = taper[:, None] * local[None, :]]
  transfers between devices with their start and end apart: 1 -> 0, of which waited for: 1 -> 0; matrix products, arithmetic and copies ran while one was open for 12% -> 0% of each run, Pallas kernels for 0% -> 0%
where the time goes in v1:
time: 18.7 us; the launch traced here: 18.6 us
  Pallas kernels  17.9 us (96%)
  between operations  0.65 us (3%)
    pallas_call x1, Pallas kernels, body(): pl.pallas_call(functools.partial(exchange, n_band, n_lev), name='exchange...  14.8 us
    pallas_call x1, Pallas kernels, body(): pl.pallas_call(functools.partial(scale, n_lev), name='scale', out_shape=(...  3.1 us

profile of v1, /device:TPU:0, one launch (start us, length us, event | category | flops | bytes accessed | tf_op | source)
XLA Modules:
  0.0 18.6 jit_solution(8350262946695877339)
XLA Ops:
  0.6 0.0 copy-start
  0.6 14.8 %exchange.1 = (bf16[34,512,128]{2,1,0:T(8,128)(2,1)S(1)}, f32[512,128]{1,0:T(8,128)S(1)}, f32[4,64,128]{2,1,0:T(8,128)S(1)}) custom-call(f32[128,128]{1,0:T(8,128)} %pattern.1, s32[128]{0:T(128)} %source_hbm.1, f32[34]{0:T(128)} %taper.1, f32[34]{0:T(128)} %thickness_hbm.1, bf16[34,512,128]{2,1,0:T(8,128)(2,1)} %bitcast.15), custom_call_target="tpu_custom_call" | custom-call | tf_op jit(solution)/shard_map/exchange/pallas_call | solution.py:175
  15.5 0.0 copy-done
  15.5 3.1 %scale.1 = (bf16[34,512,128]{2,1,0:T(8,128)(2,1)}, f32[128,2,128]{2,1,0:T(2,128)}) custom-call(f32[34]{0:T(128)S(1)} %copy-done, bf16[34,512,128]{2,1,0:T(8,128)(2,1)S(1)} %get-tuple-element.7.held, f32[512,128]{1,0:T(8,128)S(1)} %get-tuple-element.8.spread, f32[4,64,128]{2,1,0:T(8,128)S(1)} %get-tuple-element.9.totals), custom_call_target="tpu_custom_call" | custom-call | tf_op jit(solution)/shard_map/scale/pallas_call | solution.py:196
Async XLA Ops:
  0.6 14.8 %copy-start = (f32[34]{0:T(128)S(1)}, f32[34]{0:T(128)}, u32[]{:S(2)}) copy-start(f32[34]{0:T(128)} %taper.1) | copy-start | bytes 412

commit v2 on v1

--- a/solution.py
+++ b/solution.py
@@ -16,13 +16,17 @@
     levels, rows, lanes = tend.shape
     blocks = pattern.shape[0]
     fields = rows // blocks
-    share, piece = blocks // n_lev, rows // n_lev
+    pieces, half = totals.shape[0], n_lev // 2
+    share, piece = blocks // pieces, rows // pieces
     pairs = n_band // 2
+    per = pieces // 2
+    side = lev // half
+    near, far = half - 1 + side, half - side
     pair, core = band // 2, band % 2
     mate = pair * 2 + 1 - core
 
     def chunk_of(step):
-        return lax.rem(lev + 1 + step, n_lev)
+        return lax.rem(step + (1 - side) * per, pieces)
 
     def load(step):
         span = pl.ds(pl.multiple_of(chunk_of(step) * piece, piece), piece)
@@ -37,7 +41,7 @@
         ((thickness_hbm, thickness), (taper_hbm, taper), (source_hbm, source)))]
     for copy in small:
         copy.start()
-    for step in range(n_lev):
+    for step in range(pieces):
         load(step).start()
 
     barrier = pltpu.get_barrier_semaphore()
@@ -46,9 +50,11 @@
         peer = lax.rem(pair + d, pairs) * 2 + core
         pl.semaphore_signal(barrier, inc=1, device_id={"band": peer}, device_id_type=MESH)
     for d in range(1, n_lev):
-        pl.semaphore_signal(barrier, inc=1, device_id={"lev": lax.rem(lev + d, n_lev)}, device_id_type=MESH)
-    own.wait()
-    pl.semaphore_wait(barrier, pairs + n_lev - 1)
+        peer = lax.rem(lev + d, n_lev)
+
+        @pl.when((lev == near) | (peer == half - 1) | (peer == half))
+        def _(peer=peer):
+            pl.semaphore_signal(barrier, inc=1, device_id={"lev": peer}, device_id_type=MESH)
 
     def direct(d):
         peer = lax.rem(pair + d, pairs) * 2 + core
@@ -62,10 +68,6 @@
         return pltpu.make_async_remote_copy(block, block, pass_sem.at[d], got_sem.at[d],
                                             device_id={"band": mate}, device_id_type=MESH)
 
-    for d in range(1, pairs):
-        direct(d).start()
-    relay(0).start()
-
     for copy in small:
         copy.wait()
     squares = thickness[0] * thickness[0]
@@ -73,46 +75,67 @@
         squares += thickness[l] * thickness[l]
 
     def give(step):
-        owner = chunk_of(step)
-        return pltpu.make_async_remote_copy(part.at[step], inbox.at[n_lev - 2 - step], part_send.at[step],
-                                            part_recv.at[n_lev - 2 - step],
-                                            device_id={"lev": owner}, device_id_type=MESH)
-
-    for step in range(n_lev):
+        return pltpu.make_async_remote_copy(part.at[step], inbox.at[lev, step % per], part_send.at[step],
+                                            part_recv.at[lev, step % per],
+                                            device_id={"lev": far if step < per else near}, device_id_type=MESH)
+
+    def got(peer, q):
+        return pltpu.make_async_remote_copy(part.at[q], inbox.at[peer, q], part_send.at[q], part_recv.at[peer, q],
+                                            device_id={"lev": peer}, device_id_type=MESH)
+
+    def publish(d, q):
+        mine = totals.at[side * per + q]
+        return pltpu.make_async_remote_copy(mine, mine, total_send.at[d, q], total_recv.at[side * per + q],
+                                            device_id={"lev": lax.rem(lev + d, n_lev)}, device_id_type=MESH)
+
+    def send(step):
+        if step < per:
+            give(step).start()
+        else:
+            pl.when(lev != near)(lambda: give(step).start())
+
+    def level_sums(step):
         load(step).wait()
         first = pl.multiple_of(chunk_of(step) * piece, piece)
         for r in range(0, piece, 64):
             def add(l, total):
                 weight = thickness[l] * taper[l]
                 return total + weight * held[l, pl.ds(first + r, 64), :].astype(jnp.float32)
-            acc[pl.ds(r, 64), :] = lax.fori_loop(0, levels, add, jnp.zeros((64, lanes), jnp.float32), unroll=2)
+            acc[pl.ds(r, 64), :] = lax.fori_loop(0, levels, add, jnp.zeros((64, lanes), jnp.float32), unroll=34)
         for k in range(2):
             part[step, k * share:(k + 1) * share, :] = acc[pl.ds(fields - 2 + k, share, stride=fields), :]
         part[step, 2 * share:, :] = jnp.full((8, lanes), squares, jnp.float32)
-        if step < n_lev - 1:
-            give(step).start()
-
-    def arrived(d):
+
+    for step in range(2):
+        level_sums(step)
+    own.wait()
+    met = jnp.where(lev == near, n_lev - 1, 2)
+    pl.semaphore_wait(barrier, pairs + met)
+    for step in range(2):
+        send(step)
+    for d in range(1, pairs):
+        direct(d).start()
+    relay(0).start()
+
+    for step in range(2, pieces):
+        level_sums(step)
+        send(step)
+
+    @pl.when(lev == near)
+    def _():
+        for q in range(per):
+            total = part[per + q]
+            for d in range(1, n_lev):
+                peer = lax.rem(lev + d, n_lev)
+                got(peer, q).wait_recv()
+                total = total + inbox[peer, q]
+            totals[side * per + q] = total[:2 * share] / jnp.sqrt(total[2 * share:2 * share + 1])
+            for d in range(1, n_lev):
+                publish(d, q).start()
+
+    for d in range(1, pairs):
         direct(d).wait_recv()
         relay(d).start()
-
-    for d in range(1, pairs):
-        arrived(d)
-
-    for step in range(n_lev - 1):
-        give(step).wait()
-    total = part[n_lev - 1]
-    for slot in range(n_lev - 1):
-        total = total + inbox[slot]
-    totals[lev] = total[:2 * share] / jnp.sqrt(total[2 * share:2 * share + 1])
-
-    def publish(d):
-        return pltpu.make_async_remote_copy(totals.at[lev], totals.at[lev], total_send.at[d], total_recv.at[d],
-                                            device_id={"lev": lax.rem(lev + d, n_lev)}, device_id_type=MESH)
-
-    for d in range(1, n_lev):
-        publish(d).start()
-
     for d in range(pairs):
         relay(d).wait()
     for d in range(1, pairs):
@@ -123,19 +146,35 @@
         acc[pl.ds(j, 1), :] = row
         return 0
 
-    lax.fori_loop(0, blocks, pick, 0, unroll=8)
+    lax.fori_loop(0, blocks, pick, 0, unroll=32)
     local = jnp.tanh(acc[0:blocks, :])
     for f in range(fields):
         spread[pl.ds(f, blocks, stride=fields), :] = local
 
-    for d in range(1, n_lev):
-        publish(d).wait()
-
-
-def scale(n_lev, taper, held, spread, totals, out, column, made, sums, out_sem, sum_sem):
+    for step in range(pieces):
+        if step < per:
+            give(step).wait_send()
+        else:
+            pl.when(lev != near)(lambda step=step: give(step).wait_send())
+
+    @pl.when(lev == near)
+    def _():
+        for q in range(per):
+            for d in range(1, n_lev):
+                publish(d, q).wait_send()
+
+    for p in range(pieces):
+        @pl.when(lev != half - 1 + p // per)
+        def _(p=p):
+            pltpu.make_async_remote_copy(totals.at[p], totals.at[p], total_send.at[0, 0], total_recv.at[p],
+                                         device_id={"lev": far}, device_id_type=MESH).wait_recv()
+
+
+def scale(taper, held, spread, totals, out, column, made, sums, out_sem, sum_sem):
     levels, rows, lanes = held.shape
     blocks = column.shape[0]
-    share, fields = blocks // n_lev, rows // blocks
+    pieces = totals.shape[0]
+    share, fields = blocks // pieces, rows // blocks
 
     def level(l, _):
         for r in range(0, rows, 64):
@@ -145,7 +184,7 @@
         return 0
 
     lax.fori_loop(0, levels, level, 0)
-    for c in range(n_lev):
+    for c in range(pieces):
         local = spread[pl.ds(c * share * fields, share, stride=fields), :]
         for k in range(2):
             sums[c * share:(c + 1) * share, k, :] = totals[c, k * share:(k + 1) * share, :] * local
@@ -164,7 +203,8 @@
     fields, levels, columns = tendencies.shape
     blocks, lanes = pattern.shape
     rows = blocks * fields
-    share, piece, pairs = blocks // n_lev, rows // n_lev, n_band // 2
+    pieces = 4
+    share, piece, pairs = blocks // pieces, rows // pieces, n_band // 2
     tend = tendencies.transpose(1, 0, 2).reshape(levels, fields, blocks, lanes)
     tend = tend.transpose(0, 2, 1, 3).reshape(levels, rows, lanes)
     anywhere = pl.BlockSpec(memory_space=pl.ANY)
@@ -176,25 +216,25 @@
         functools.partial(exchange, n_band, n_lev),
         name="exchange",
         out_shape=(pltpu.VMEM(tend.shape, tend.dtype), pltpu.VMEM((rows, lanes), f32),
-                   pltpu.VMEM((n_lev, 2 * share, lanes), f32)),
+                   pltpu.VMEM((pieces, 2 * share, lanes), f32)),
         in_specs=[hbm] * 5,
         out_specs=(vector, vector, vector),
         scratch_shapes=[
             pltpu.VMEM((n_band * blocks, lanes), f32),
             pltpu.VMEM((max(piece, blocks), lanes), f32),
-            pltpu.VMEM((n_lev, 2 * share + 8, lanes), f32),
-            pltpu.VMEM((n_lev - 1, 2 * share + 8, lanes), f32),
+            pltpu.VMEM((pieces, 2 * share + 8, lanes), f32),
+            pltpu.VMEM((n_lev, pieces // 2, 2 * share + 8, lanes), f32),
             pltpu.SMEM(block_source.shape, jnp.int32), pltpu.SMEM(taper.shape, f32),
             pltpu.SMEM(thickness.shape, f32), dma((3,)),
-            dma, dma((n_lev,)), dma((pairs,)), dma((pairs,)), dma((pairs,)), dma((pairs,)),
-            dma((n_lev,)), dma((n_lev,)), dma((n_lev,)), dma((n_lev,)),
+            dma, dma((pieces,)), dma((pairs,)), dma((pairs,)), dma((pairs,)), dma((pairs,)),
+            dma((pieces,)), dma((n_lev, pieces // 2)), dma((n_lev, pieces // 2)), dma((pieces,)),
         ],
         compiler_params=pltpu.CompilerParams(collective_id=0, has_side_effects=True, vmem_limit_bytes=12 << 20),
     )(*(pltpu.with_memory_space_constraint(x, pltpu.MemorySpace.HBM)
         for x in (pattern, block_source, taper, thickness, tend)))
     in_vmem = lambda x: pltpu.with_memory_space_constraint(x, pltpu.MemorySpace.VMEM)
     out, column = pl.pallas_call(
-        functools.partial(scale, n_lev),
+        scale,
         name="scale",
         out_shape=(jax.ShapeDtypeStruct(tend.shape, tend.dtype), jax.ShapeDtypeStruct((blocks, 2, lanes), f32)),
         in_specs=[scalars, vector, vector, vector],

time: 18.7 us -> 18.3 us (0.979)
  Pallas kernels: 17.9 us -> 17.5 us
    pallas_call x1, Pallas kernels: 14.8 us -> 14.4 us  [body(): pl.pallas_call(functools.partial(exchange, n_band, n_lev), name='exchange...]
where the time goes in v2:
time: 18.3 us; the launch traced here: 18.1 us
  Pallas kernels  17.5 us (96%)
  between operations  0.65 us (4%)
    pallas_call x1, Pallas kernels, body(): pl.pallas_call(functools.partial(exchange, n_band, n_lev), name='exchange...  14.4 us
    pallas_call x1, Pallas kernels, body(): pl.pallas_call(scale, name='scale', out_shape=(jax.ShapeDtypeStruct(tend....  3.1 us

profile of v2, /device:TPU:0, one launch (start us, length us, event | category | flops | bytes accessed | tf_op | source)
XLA Modules:
  0.0 18.1 jit_solution(2601232060310458265)
XLA Ops:
  0.6 0.0 copy-start
  0.6 14.4 %exchange.1 = (bf16[34,512,128]{2,1,0:T(8,128)(2,1)S(1)}, f32[512,128]{1,0:T(8,128)S(1)}, f32[4,64,128]{2,1,0:T(8,128)S(1)}) custom-call(f32[128,128]{1,0:T(8,128)} %pattern.1, s32[128]{0:T(128)} %source_hbm.1, f32[34]{0:T(128)} %taper.1, f32[34]{0:T(128)} %thickness_hbm.1, bf16[34,512,128]{2,1,0:T(8,128)(2,1)} %bitcast.15), custom_call_target="tpu_custom_call" | custom-call | tf_op jit(solution)/shard_map/exchange/pallas_call | solution.py:215
  15.0 0.0 copy-done
  15.0 3.1 %scale.1 = (bf16[34,512,128]{2,1,0:T(8,128)(2,1)}, f32[128,2,128]{2,1,0:T(2,128)}) custom-call(f32[34]{0:T(128)S(1)} %copy-done, bf16[34,512,128]{2,1,0:T(8,128)(2,1)S(1)} %get-tuple-element.7.held, f32[512,128]{1,0:T(8,128)S(1)} %get-tuple-element.8.spread, f32[4,64,128]{2,1,0:T(8,128)S(1)} %get-tuple-element.9.totals), custom_call_target="tpu_custom_call" | custom-call | tf_op jit(solution)/shard_map/scale/pallas_call | solution.py:236
Async XLA Ops:
  0.6 14.4 %copy-start = (f32[34]{0:T(128)S(1)}, f32[34]{0:T(128)}, u32[]{:S(2)}) copy-start(f32[34]{0:T(128)} %taper.1) | copy-start | bytes 412

commit v3 on v2

--- a/solution.py
+++ b/solution.py
@@ -26,7 +26,8 @@
     mate = pair * 2 + 1 - core
 
     def chunk_of(step):
-        return lax.rem(step + (1 - side) * per, pieces)
+        owner = 1 - side if step % 2 == 0 else side
+        return owner * per + step // 2
 
     def load(step):
         span = pl.ds(pl.multiple_of(chunk_of(step) * piece, piece), piece)
@@ -75,9 +76,9 @@
         squares += thickness[l] * thickness[l]
 
     def give(step):
-        return pltpu.make_async_remote_copy(part.at[step], inbox.at[lev, step % per], part_send.at[step],
-                                            part_recv.at[lev, step % per],
-                                            device_id={"lev": far if step < per else near}, device_id_type=MESH)
+        return pltpu.make_async_remote_copy(part.at[step], inbox.at[lev, step // 2], part_send.at[step],
+                                            part_recv.at[lev, step // 2],
+                                            device_id={"lev": far if step % 2 == 0 else near}, device_id_type=MESH)
 
     def got(peer, q):
         return pltpu.make_async_remote_copy(part.at[q], inbox.at[peer, q], part_send.at[q], part_recv.at[peer, q],
@@ -89,7 +90,7 @@
                                             device_id={"lev": lax.rem(lev + d, n_lev)}, device_id_type=MESH)
 
     def send(step):
-        if step < per:
+        if step % 2 == 0:
             give(step).start()
         else:
             pl.when(lev != near)(lambda: give(step).start())
@@ -104,7 +105,7 @@
             acc[pl.ds(r, 64), :] = lax.fori_loop(0, levels, add, jnp.zeros((64, lanes), jnp.float32), unroll=34)
         for k in range(2):
             part[step, k * share:(k + 1) * share, :] = acc[pl.ds(fields - 2 + k, share, stride=fields), :]
-        part[step, 2 * share:, :] = jnp.full((8, lanes), squares, jnp.float32)
+        part[step, 2 * share:, :] = jnp.full((1, lanes), squares, jnp.float32)
 
     for step in range(2):
         level_sums(step)
@@ -124,7 +125,7 @@
     @pl.when(lev == near)
     def _():
         for q in range(per):
-            total = part[per + q]
+            total = part[2 * q + 1]
             for d in range(1, n_lev):
                 peer = lax.rem(lev + d, n_lev)
                 got(peer, q).wait_recv()
@@ -152,7 +153,7 @@
         spread[pl.ds(f, blocks, stride=fields), :] = local
 
     for step in range(pieces):
-        if step < per:
+        if step % 2 == 0:
             give(step).wait_send()
         else:
             pl.when(lev != near)(lambda step=step: give(step).wait_send())
@@ -222,8 +223,8 @@
         scratch_shapes=[
             pltpu.VMEM((n_band * blocks, lanes), f32),
             pltpu.VMEM((max(piece, blocks), lanes), f32),
-            pltpu.VMEM((pieces, 2 * share + 8, lanes), f32),
-            pltpu.VMEM((n_lev, pieces // 2, 2 * share + 8, lanes), f32),
+            pltpu.VMEM((pieces, 2 * share + 1, lanes), f32),
+            pltpu.VMEM((n_lev, pieces // 2, 2 * share + 1, lanes), f32),
             pltpu.SMEM(block_source.shape, jnp.int32), pltpu.SMEM(taper.shape, f32),
             pltpu.SMEM(thickness.shape, f32), dma((3,)),
             dma, dma((pieces,)), dma((pairs,)), dma((pairs,)), dma((pairs,)), dma((pairs,)),

time: 18.3 us -> 17.7 us (0.967)
  Pallas kernels: 17.5 us -> 16.9 us
    pallas_call x1, Pallas kernels: 14.4 us -> 13.8 us  [body(): pl.pallas_call(functools.partial(exchange, n_band, n_lev), name='exchange...]
where the time goes in v3:
time: 17.7 us; the launch traced here: 17.5 us
  Pallas kernels  16.9 us (95%)
  between operations  0.65 us (4%)
    pallas_call x1, Pallas kernels, body(): pl.pallas_call(functools.partial(exchange, n_band, n_lev), name='exchange...  13.8 us
    pallas_call x1, Pallas kernels, body(): pl.pallas_call(scale, name='scale', out_shape=(jax.ShapeDtypeStruct(tend....  3.1 us

profile of v3, /device:TPU:0, one launch (start us, length us, event | category | flops | bytes accessed | tf_op | source)
XLA Modules:
  0.0 17.5 jit_solution(6873664721728695514)
XLA Ops:
  0.6 0.0 copy-start
  0.6 13.8 %exchange.1 = (bf16[34,512,128]{2,1,0:T(8,128)(2,1)S(1)}, f32[512,128]{1,0:T(8,128)S(1)}, f32[4,64,128]{2,1,0:T(8,128)S(1)}) custom-call(f32[128,128]{1,0:T(8,128)} %pattern.1, s32[128]{0:T(128)} %source_hbm.1, f32[34]{0:T(128)} %taper.1, f32[34]{0:T(128)} %thickness_hbm.1, bf16[34,512,128]{2,1,0:T(8,128)(2,1)} %bitcast.15), custom_call_target="tpu_custom_call" | custom-call | tf_op jit(solution)/shard_map/exchange/pallas_call | solution.py:216
  14.4 0.0 copy-done
  14.4 3.1 %scale.1 = (bf16[34,512,128]{2,1,0:T(8,128)(2,1)}, f32[128,2,128]{2,1,0:T(2,128)}) custom-call(f32[34]{0:T(128)S(1)} %copy-done, bf16[34,512,128]{2,1,0:T(8,128)(2,1)S(1)} %get-tuple-element.7.held, f32[512,128]{1,0:T(8,128)S(1)} %get-tuple-element.8.spread, f32[4,64,128]{2,1,0:T(8,128)S(1)} %get-tuple-element.9.totals), custom_call_target="tpu_custom_call" | custom-call | tf_op jit(solution)/shard_map/scale/pallas_call | solution.py:237
Async XLA Ops:
  0.6 13.8 %copy-start = (f32[34]{0:T(128)S(1)}, f32[34]{0:T(128)}, u32[]{:S(2)}) copy-start(f32[34]{0:T(128)} %taper.1) | copy-start | bytes 412
